TPU v7x, 128 devices: a whole 4x4x4 slice. The times are simulated.
128 devices in a mesh: segment: 2 (over core), mp: 64 (over x, y, z).
Axes of the slice: x: 4, y: 4, z: 4, core: 2. Of those that a mesh axis runs over, the one named last changes fastest.
Arguments:
- tokens: float32 [2, 128, 1024], P(None, 'mp'), may hold values from -6 to 6
- curvature: float32 [2, 128, 1024], P(None, 'mp'), may hold values from 0.05 to 0.5
- gains: float32 [2, 1024], P('segment'), may hold values from 0.1 to 1.9
- w_in: float32 [2, 1024, 65536], P('segment', None, 'mp'), may hold values from -0.1875 to 0.1875
- w_out: float32 [2, 65536, 1024], P('segment', 'mp'), may hold values from -0.0234375 to 0.0234375
- v_in: float32 [2, 1024, 65536], P('segment', None, 'mp'), may hold values from -0.1875 to 0.1875
- v_out: float32 [2, 65536, 1024], P('segment', 'mp'), may hold values from -0.0234375 to 0.0234375
Outputs:
- product_in: float32 [2, 1024, 65536], P('segment', None, 'mp')
- product_out: float32 [2, 65536, 1024], P('segment', 'mp')
All inputs are finite; a program needn't handle non-finite values.
Results may differ from a plain program's by a relative error of at most 0.00011.
Values sent between devices are 32-bit elements; how exact they have to be, the bound alone decides.
No kernel may reach another device: no remote copies, remote signals or barrier semaphores. Data moves between devices by JAX's collectives and lax.ppermute only.
A program may use at most 128 MiB of HBM per device.

v0:
```python
import functools

import jax
import jax.numpy as jnp
from jax import lax
from jax.experimental import pallas as pl
from jax.experimental.pallas import tpu as pltpu
from jax.sharding import PartitionSpec as P

eps = 1e-06
coeff = 0.7978845608028654
f32 = jnp.float32
bf16 = jnp.bfloat16
UNITS = 256
MIB = 1 << 20


def gelu_pair(h):
    inner = coeff * (h + 0.044715 * h * h * h)
    tval = jnp.tanh(inner)
    act = 0.5 * h * (1.0 + tval)
    slope = 0.5 * (1.0 + tval) + 0.5 * h * (1.0 - tval * tval) * coeff * (
        1.0 + 3.0 * 0.044715 * h * h
    )
    return act, slope


def mean(v):
    return jnp.mean(v, axis=-1, keepdims=True)


def parts(v):
    high = v.astype(bf16)
    return high, (v - high.astype(f32)).astype(bf16)


def dot3(a, b, ca=1, cb=0):
    dims = (((ca,), (cb,)), ((), ()))

    def one(x, y):
        return lax.dot_general(x, y, dims, preferred_element_type=f32)

    return one(a[0], b[0]) + one(a[1], b[0]) + one(a[0], b[1])


def to_block(rows):
    half = rows.shape[1] // 2
    return jnp.concatenate([rows[:, :half], rows[:, half:]], axis=0)


def from_block(block):
    rows = block.shape[0] // 2
    return jnp.concatenate([block[:rows], block[rows:]], axis=1)


def swap_halves(left, right):
    top = lax.broadcasted_iota(jnp.int32, left.shape, 1) < 4
    return (
        jnp.where(top, left, pltpu.roll(right, 4, 1)),
        jnp.where(top, pltpu.roll(left, 4, 1), right),
    )


def store_blocks(out_ref, at, whole):
    half = whole.shape[1] // 2
    pairs = whole.reshape(whole.shape[0] // 8, 8, whole.shape[1])
    even, odd = swap_halves(pairs[:, :, :half], pairs[:, :, half:])
    both = jnp.stack([even, odd], axis=1)
    out_ref[:, :, at : at + half] = both.reshape(2 * pairs.shape[0], 8, half)


def load_blocks(ref, at, half):
    blocks = ref[:, :, at : at + half]
    pairs = blocks.reshape(blocks.shape[0] // 2, 2, 8, half)
    left, right = swap_halves(pairs[:, 0], pairs[:, 1])
    whole = jnp.concatenate([left, right], axis=2)
    return whole.reshape(whole.shape[0] * 8, 2 * half)


def call(body, out, grid=None, ins=None, outs=None, scratch=(), flops=0, moved=0, name=None):
    kwargs = {}
    if grid is not None:
        kwargs = dict(grid=grid, in_specs=ins, out_specs=outs)
    return pl.pallas_call(
        body,
        out_shape=out,
        scratch_shapes=list(scratch),
        compiler_params=pltpu.CompilerParams(vmem_limit_bytes=40 * MIB),
        cost_estimate=pl.CostEstimate(flops=flops, bytes_accessed=moved, transcendentals=0),
        name=name,
        **kwargs,
    )


def struct(*shape, dtype=f32):
    return jax.ShapeDtypeStruct(shape, dtype)


def full(*shape):
    return pl.BlockSpec(shape, lambda j: (0,) * len(shape))


def spread_first(tok_ref, gain_ref, out_ref):
    x = tok_ref[...]
    n = x * lax.rsqrt(mean(x * x) + eps) * gain_ref[...]
    out_ref[...] = jnp.broadcast_to(to_block(n), out_ref.shape)


def spread(row_ref, out_ref):
    out_ref[...] = jnp.broadcast_to(to_block(row_ref[...]), out_ref.shape)


def spread_last(row_ref, gain_ref, out_ref):
    width = gain_ref.shape[1]
    x = row_ref[:, :width]
    dx = row_ref[:, width:]
    r = lax.rsqrt(mean(x * x) + eps)
    n = x * r * gain_ref[...]
    dn = gain_ref[...] * (dx * r - x * r**3 * mean(x * dx))
    half = width // 2
    out_ref[:, :, :half] = jnp.broadcast_to(to_block(n), (out_ref.shape[0], 8, half))
    out_ref[:, :, half:] = jnp.broadcast_to(to_block(dn), (out_ref.shape[0], 8, half))


def sum_first(blocks_ref, tok_ref, out_ref):
    total = jnp.sum(blocks_ref[...], axis=0)
    half = total.shape[1] // 2
    width = tok_ref.shape[1]
    out_ref[:, :width] = tok_ref[...] + from_block(total[:, :half])
    out_ref[:, width:] = from_block(total[:, half:])


def sum_last(blocks_ref, row_ref, curv_ref, rows_ref, out_ref):
    width = curv_ref.shape[1]
    g = curv_ref[...] * (row_ref[:, width:] + from_block(jnp.sum(blocks_ref[...], axis=0)))
    rows_ref[...] = g
    out_ref[...] = jnp.broadcast_to(to_block(g), out_ref.shape)


def sum_back(blocks_ref, g_ref, row_ref, gain_ref, out_ref):
    width = gain_ref.shape[1]
    u = gain_ref[...] * from_block(jnp.sum(blocks_ref[...], axis=0))
    x = row_ref[:, :width]
    r = lax.rsqrt(mean(x * x) + eps)
    out_ref[...] = g_ref[...] + u * r - x * r**3 * mean(x * u)


def forward(last, blocks_ref, wi_ref, vi_ref, wo_ref, vo_ref, out_ref, nh_ref, nl_ref, ah_ref, al_ref, p_ref, d_ref, *sums):
    j = pl.program_id(0)
    half = nh_ref.shape[1] // 2

    @pl.when(j == 0)
    def _():
        nh_ref[...], nl_ref[...] = parts(load_blocks(blocks_ref, 0, half))
        if last:
            d_ref[0], d_ref[1] = parts(load_blocks(blocks_ref, half, half))

    n = nh_ref[...], nl_ref[...]
    wi = parts(wi_ref[...])
    h = dot3(n, wi)
    dh = dot3(n, parts(vi_ref[...]))
    if last:
        dh = dh + dot3((d_ref[0], d_ref[1]), wi)
    act, slope = gelu_pair(h)
    p_ref[...] = slope
    a = parts(act)
    ah_ref[...], al_ref[...] = a
    da = parts(slope * dh)
    wo = parts(wo_ref[...])
    terms = [dot3(da, wo) + dot3(a, parts(vo_ref[...]))]
    if not last:
        terms.insert(0, dot3(a, wo))
    for sum_ref, term in zip(sums, terms):

        @pl.when(j == 0)
        def _():
            sum_ref[...] = term

        @pl.when(j > 0)
        def _():
            sum_ref[...] += term

    @pl.when(j == pl.num_programs(0) - 1)
    def _():
        for k, sum_ref in enumerate(sums):
            store_blocks(out_ref, k * half, sum_ref[...])


def run_forward(blocks, wi, vi, wo, vo, last):
    chips, _, lanes = blocks.shape
    width, units = wi.shape
    rows = chips * 4
    steps = units // UNITS
    sums = 1 if last else 2
    out_lanes = sums * width // 2
    inward = pl.BlockSpec((width, UNITS), lambda j: (0, j))
    outward = pl.BlockSpec((UNITS, width), lambda j: (j, 0))
    held = pl.BlockSpec((rows, UNITS), lambda j: (0, j))
    return call(
        functools.partial(forward, last),
        (
            struct(chips, 8, out_lanes),
            struct(rows, width, dtype=bf16),
            struct(rows, width, dtype=bf16),
            struct(rows, units, dtype=bf16),
            struct(rows, units, dtype=bf16),
            struct(rows, units),
        ),
        grid=(steps,),
        ins=[full(chips, 8, lanes), inward, inward, outward, outward],
        outs=(full(chips, 8, out_lanes), full(rows, width), full(rows, width), held, held, held),
        scratch=[pltpu.VMEM((2, rows, width) if last else (2, 8, 128), bf16)]
        + [pltpu.VMEM((rows, width), f32)] * sums,
        flops=2 * rows * width * units * 5 * 3,
        moved=4 * width * units * 4,
        name="forward_last" if last else "forward_first",
    )(blocks, wi, vi, wo, vo)


def backward(with_input, blocks_ref, p_ref, wo_ref, *refs):
    if with_input:
        wi_ref, gh_ref, gl_ref, eh_ref, el_ref, out_ref, u_ref = refs
    else:
        gh_ref, gl_ref, eh_ref, el_ref = refs
    j = pl.program_id(0)
    half = gh_ref.shape[1] // 2

    @pl.when(j == 0)
    def _():
        gh_ref[...], gl_ref[...] = parts(load_blocks(blocks_ref, 0, half))

    g = gh_ref[...], gl_ref[...]
    e = parts(p_ref[...] * dot3(g, parts(wo_ref[...]), 1, 1))
    eh_ref[...], el_ref[...] = e
    if with_input:
        u = dot3(e, parts(wi_ref[...]), 1, 1)

        @pl.when(j == 0)
        def _():
            u_ref[...] = u

        @pl.when(j > 0)
        def _():
            u_ref[...] += u

        @pl.when(j == pl.num_programs(0) - 1)
        def _():
            store_blocks(out_ref, 0, u_ref[...])


def run_backward(blocks, p, wo, wi=None):
    chips, _, lanes = blocks.shape
    units, width = wo.shape
    rows = chips * 4
    inward = pl.BlockSpec((width, UNITS), lambda j: (0, j))
    outward = pl.BlockSpec((UNITS, width), lambda j: (j, 0))
    held = pl.BlockSpec((rows, UNITS), lambda j: (0, j))
    more = wi is not None
    whole = full(rows, width)
    return call(
        functools.partial(backward, more),
        (
            struct(rows, width, dtype=bf16),
            struct(rows, width, dtype=bf16),
            struct(rows, units, dtype=bf16),
            struct(rows, units, dtype=bf16),
        )
        + ((struct(chips, 8, lanes),) if more else ()),
        grid=(units // UNITS,),
        ins=[full(chips, 8, lanes), held, outward] + ([inward] if more else []),
        outs=(whole, whole, held, held) + ((full(chips, 8, lanes),) if more else ()),
        scratch=[pltpu.VMEM((rows, width), f32)] if more else [],
        flops=2 * rows * width * units * 3 * (2 if more else 1),
        moved=4 * width * units * (2 if more else 1),
        name="backward_last" if more else "backward_first",
    )(*((blocks, p, wo) + ((wi,) if more else ())))


def products(nh_ref, nl_ref, ah_ref, al_ref, eh_ref, el_ref, gh_ref, gl_ref, in_ref, out_ref):
    out_ref[...] = dot3((ah_ref[...], al_ref[...]), (gh_ref[...], gl_ref[...]), 0, 0)
    in_ref[...] = dot3((nh_ref[...], nl_ref[...]), (eh_ref[...], el_ref[...]), 0, 0)


def run_products(n, a, e, g):
    rows, width = n[0].shape
    units = a[0].shape[1]
    held = pl.BlockSpec((rows, UNITS), lambda j: (0, j))
    whole = full(rows, width)
    return call(
        products,
        (struct(width, units), struct(units, width)),
        grid=(units // UNITS,),
        ins=[whole, whole, held, held, held, held, whole, whole],
        outs=(
            pl.BlockSpec((width, UNITS), lambda j: (0, j)),
            pl.BlockSpec((UNITS, width), lambda j: (j, 0)),
        ),
        flops=2 * rows * width * units * 6,
        moved=8 * width * units,
        name="products",
    )(*n, *a, *e, *g)


def exchanged(blocks):
    return lax.all_to_all(blocks, "mp", 0, 0, tiled=True)


def on_device(tokens, curvature, gains, w_in, w_out, v_in, v_out):
    first = lax.axis_index("segment") == 0
    gain, wi, wo, vi, vo = gains, w_in[0], w_out[0], v_in[0], v_out[0]
    width = tokens.shape[2]
    x0 = tokens.reshape(-1, width)
    curv = curvature.reshape(-1, width)
    rows = x0.shape[0]
    chips = lax.axis_size("mp")
    total = rows * chips
    units = wi.shape[1]
    single = struct(chips, 8, width // 2)
    double = struct(chips, 8, width)

    def blank(*shape, dtype=f32):
        return jnp.zeros(shape, dtype)

    def blanks(count, columns):
        return tuple(blank(total, columns, dtype=bf16) for _ in range(count))

    def forward_first():
        blocks = exchanged(call(spread_first, single, name="spread_first")(x0, gain))
        out, nh, nl, ah, al, p = run_forward(blocks, wi, vi, wo, vo, False)
        rows_out = call(sum_first, struct(rows, 2 * width), name="sum_first")(exchanged(out), x0)
        return rows_out, nh, nl, ah, al, p

    def no_forward():
        return (blank(rows, 2 * width), *blanks(2, width), *blanks(2, units), blank(total, units))

    both, *held = lax.cond(first, forward_first, no_forward)
    p0 = held.pop()
    both = lax.ppermute(both, "segment", [(0, 1)])

    def layer_last(both, *held):
        blocks = exchanged(call(spread_last, double, name="spread_last")(both, gain))
        out, nh, nl, ah, al, p = run_forward(blocks, wi, vi, wo, vo, True)
        g, blocks = call(sum_last, (struct(rows, width), single), name="sum_last")(
            exchanged(out), both, curv
        )
        gh, gl, eh, el, out = run_backward(exchanged(blocks), p, wo, wi)
        back = call(sum_back, struct(rows, width), name="sum_back")(exchanged(out), g, both, gain)
        return back, nh, nl, ah, al, eh, el, gh, gl

    def keep(both, *held):
        return (blank(rows, width), *held, *blanks(2, units), *blanks(2, width))

    back, nh, nl, ah, al, *rest = lax.cond(first, keep, layer_last, both, *held)
    back = lax.ppermute(back, "segment", [(1, 0)])

    def backward_first(back, *rest):
        blocks = exchanged(call(spread, single, name="spread")(back))
        gh, gl, eh, el = run_backward(blocks, p0, wo)
        return eh, el, gh, gl

    def pass_on(back, *rest):
        return rest

    eh, el, gh, gl = lax.cond(first, backward_first, pass_on, back, *rest)

    product_in, product_out = run_products((nh, nl), (ah, al), (eh, el), (gh, gl))
    return product_in[None], product_out[None]


def solution(mesh):
    rows = P(None, "mp", None)
    layer_in = P("segment", None, "mp")
    layer_out = P("segment", "mp", None)
    return jax.shard_map(
        on_device,
        mesh=mesh,
        in_specs=(rows, rows, P("segment", None), layer_in, layer_out, layer_in, layer_out),
        out_specs=(layer_in, layer_out),
        check_vma=False,
    )
```

profile of v0, /device:TPU:0, one launch (start us, length us, event | category | flops | bytes accessed | tf_op | source)
XLA Modules:
  0.0 210.7 jit_solution(15882793514080946171)
XLA Ops:
  0.6 0.0 copy-start.2
  0.6 66.2 %conditional.3 = (f32[4,2048]{1,0:T(4,128)S(1)}, bf16[256,1024]{1,0:T(8,128)(2,1)}, bf16[256,1024]{1,0:T(8,128)(2,1)}, bf16[256,1024]{1,0:T(8,128)(2,1)}, bf16[2...) conditional(s32[]{:T(128)} %convert_element_type.2, () %tuple.31, (f32[2,2,1024]{2,1,0:T(2,128)}, ...), branch_computations={%region_0.0_spmd, %region_1.0_spmd} | conditional | flops 8053063680 | bytes 23101488 | solution.py:336
  0.7 0.7 reshape.10.tok_ref
  1.4 0.9 spread_first.1
  2.3 25.7 %all_to_all.28.blocks_ref = f32[64,8,512]{2,1,0:T(8,128)S(1)} all-to-all(f32[64,8,512]{2,1,0:T(8,128)S(1)} %spread_first.1), channel_id=1, replica_groups=mesh['segment'=2,'mp'=64] {'mp'}, dimensions={0} | all-to-all | bytes 2097152 | tf_op jit(solution)/shard_map/cond/branch_1_fun/all_to_all | solution.py:305
  27.9 14.5 %forward_first.1 = (f32[64,8,1024]{2,1,0:T(8,128)S(1)}, bf16[256,1024]{1,0:T(8,128)(2,1)}, bf16[256,1024]{1,0:T(8,128)(2,1)}, bf16[256,1024]{1,0:T(8,128)(2,1)},...) custom-call(f32[64,8,512]{2,1,0:T(8,128)S(1)} %all_to_all.28.blocks_ref, f32[1024,1024]{1,0:T(8,128)} %get-tuple-element.52.wi_ref, ...), custom_call_target="tpu_custom_call" | custom-call | flops 8053063680 | bytes 16777216 | tf_op jit(solution)/shard_map/cond/branch_1_fun/forward_first/pallas_call | solution.py:199
  42.4 24.3 %all_to_all.29.blocks_ref = f32[64,8,1024]{2,1,0:T(8,128)S(1)} all-to-all(f32[64,8,1024]{2,1,0:T(8,128)S(1)} %get-tuple-element.56), channel_id=1, replica_groups=mesh['segment'=2,'mp'=64] {'mp'}, dimensions={0} | all-to-all | bytes 4194304 | tf_op jit(solution)/shard_map/cond/branch_1_fun/all_to_all | solution.py:305
  66.7 0.1 sum_first.1
  66.9 1.3 collective-permute-start
  68.2 0.8 collective-permute-done
  69.0 0.0 copy-done.2
  69.0 1.8 conditional.4
  69.0 0.1 broadcast.14.clone.2
  69.1 0.1 broadcast.14.clone.1
  69.1 0.9 broadcast.14.clone
  70.0 0.9 broadcast.14
  70.9 1.3 collective-permute-start.1
  72.1 107.0 %collective-permute-done.1 = f32[4,1024]{1,0:T(4,128)S(1)} collective-permute-done((f32[4,1024]{1,0:T(4,128)S(1)}, f32[4,1024]{1,0:T(4,128)S(1)}, u32[]{:S(2)}, u32[]{:S(2)}) %collective-permute-start.1) | collective-permute-done | bytes 16416 | tf_op jit(solution)/shard_map/ppermute | solution.py:354
  179.2 24.4 %conditional.5 = ((bf16[256,1024]{1,0:T(8,128)(2,1)}, bf16[256,1024]{1,0:T(8,128)(2,1)}, bf16[256,1024]{1,0:T(8,128)(2,1)S(1)}, bf16[256,1024]{1,0:T(8,128)(2,1)S(1)})) conditional(s32[]{:T(128)} %convert_element_type.2, (bf16[256,1024]{1,0:T(8,128)(2,1)}, bf16[256,1024]{1,0:T(8,128)(2,1)}, bf16[256,1024]{1,0:T(8,128)(2,1)S(1)}, ...), branch_computations={%region_4.0_spmd, %region_5.0_spmd} | conditional | flops 1610612736 | bytes 6291496 | solution.py:364
  179.2 0.1 spread.1
  179.3 18.8 %all_to_all.33.blocks_ref = f32[64,8,512]{2,1,0:T(8,128)S(1)} all-to-all(f32[64,8,512]{2,1,0:T(8,128)S(1)} %spread.1), channel_id=1, replica_groups=mesh['segment'=2,'mp'=64] {'mp'}, dimensions={0} | all-to-all | bytes 2097152 | tf_op jit(solution)/shard_map/cond/branch_1_fun/all_to_all | solution.py:305
  198.1 5.5 %backward_first.1 = (bf16[256,1024]{1,0:T(8,128)(2,1)S(1)}, bf16[256,1024]{1,0:T(8,128)(2,1)S(1)}, bf16[256,1024]{1,0:T(8,128)(2,1)}, bf16[256,1024]{1,0:T(8,128)(2,1)}) custom-call(f32[64,8,512]{2,1,0:T(8,128)S(1)} %all_to_all.33.blocks_ref, f32[256,1024]{1,0:T(8,128)S(1)} %get-tuple-element.87.p_ref, f32[1024,1024]{1,0:T(8,128)} %get-tuple-element.88.wo_ref), custom_call_target="tpu_custom_call" | custom-call | flops 1610612736 | bytes 4194304 | tf_op jit(solution)/shard_map/cond/branch_1_fun/backward_first/pallas_call | solution.py:260
  203.6 7.1 %products.1 = (f32[1024,1024]{1,0:T(8,128)}, f32[1024,1024]{1,0:T(8,128)}) custom-call(bf16[256,1024]{1,0:T(8,128)(2,1)} %get-tuple-element.121.nh_ref, bf16[256,1024]{1,0:T(8,128)(2,1)} %get-tuple-element.122.nl_ref, bf16[256,1024]{1,0:T(8,128)(2,1)} %get-tuple-element.123.ah_ref, bf16[256,1024]{1,0:T(8,128)(2,1)} %get-tuple-element.124.al_ref, ...), custom_call_target="tpu_custom_call" | custom-call | flops 3221225472 | bytes 8388608 | tf_op jit(solution)/shard_map/products/pallas_call | solution.py:289
  (1 shorter events, 0.0 us)
Async XLA Ops:
  0.6 68.4 %copy-start.2 = (f32[2,2,1024]{2,1,0:T(2,128)S(1)}, f32[2,2,1024]{2,1,0:T(2,128)}, u32[]{:S(2)}) copy-start(f32[2,2,1024]{2,1,0:T(2,128)} %param.14) | copy-start | bytes 49156
  66.9 2.1 %collective-permute-start = (f32[4,2048]{1,0:T(4,128)S(1)}, f32[4,2048]{1,0:T(4,128)S(1)}, u32[]{:S(2)}, u32[]{:S(2)}) collective-permute-start(f32[4,2048]{1,0:T(4,128)S(1)} %get-tuple-element.116), channel_id=1, source_target_pairs={{0,64},{1,65},{2,66},{3,67},{4,68},{5,69},{6,70},{7,71},{8,72},{9,... | collective-permute-start | bytes 98312 | tf_op jit(solution)/shard_map/ppermute | solution.py:338
  70.9 108.3 %collective-permute-start.1 = (f32[4,1024]{1,0:T(4,128)S(1)}, f32[4,1024]{1,0:T(4,128)S(1)}, u32[]{:S(2)}, u32[]{:S(2)}) collective-permute-start(f32[4,1024]{1,0:T(4,128)S(1)} %get-tuple-element.129), channel_id=1, source_target_pairs={{64,0},{65,1},{66,2},{67,3},{68,4},{69,5},{70,6},{71,7},{72,8},{73... | collective-permute-start | bytes 49160 | tf_op jit(solution)/shard_map/ppermute | solution.py:354
where the time goes:
time: 211 us
  waiting for transfers between devices  108 us (51%)
  blocking collectives  68.8 us (33%)
  Pallas kernels  28.1 us (13%)
  local copies, waits for them, and re-layouts  2.57 us (1%)
  starting transfers between devices  2.57 us (1%)
    ppermute x1, waiting for transfers between devices, on_device(): back = lax.ppermute(back, 'segment', [(1, 0)])  107 us
    all_to_all x3, blocking collectives, exchanged(): return lax.all_to_all(blocks, 'mp', 0, 0, tiled=True)  68.8 us
    pallas_call x1, Pallas kernels, run_forward(): call(functools.partial(forward, last), (struct(chips, 8, out_lanes), stru...  14.5 us
    pallas_call x1, Pallas kernels, run_products(): call(products, (struct(width, units), struct(units, width)), grid=(units...  7.08 us
    pallas_call x1, Pallas kernels, run_backward(): call(functools.partial(backward, more), (struct(rows, width, dtype=bf16),...  5.49 us
  transfers between devices with their start and end apart: 2, of which 2 were waited for; matrix products, arithmetic and copies ran while one was open for 0% of the time, Pallas kernels for 0%

commit v1 on v0

v1 whole, which is shorter than its diff:
```python
import functools

import jax
import jax.numpy as jnp
from jax import lax
from jax.experimental import pallas as pl
from jax.experimental.pallas import tpu as pltpu
from jax.sharding import PartitionSpec as P

eps = 1e-06
coeff = 0.7978845608028654
f32 = jnp.float32
bf16 = jnp.bfloat16
UNITS = 256
MIB = 1 << 20
LANES = 128
GROUP = 4
PIECES = 2
COVER_FLOPS = 1 << 34


def gelu_pair(h):
    inner = coeff * (h + 0.044715 * h * h * h)
    tval = jnp.tanh(inner)
    act = 0.5 * h * (1.0 + tval)
    slope = 0.5 * (1.0 + tval) + 0.5 * h * (1.0 - tval * tval) * coeff * (
        1.0 + 3.0 * 0.044715 * h * h
    )
    return act, slope


def mean(v):
    return jnp.mean(v, axis=-1, keepdims=True)


def parts(v):
    high = v.astype(bf16)
    return high, (v - high.astype(f32)).astype(bf16)


def dot3(a, b, ca=1, cb=0):
    dims = (((ca,), (cb,)), ((), ()))

    def one(x, y):
        return lax.dot_general(x, y, dims, preferred_element_type=f32)

    return one(a[0], b[0]) + one(a[1], b[0]) + one(a[0], b[1])


def to_block(rows):
    half = rows.shape[1] // 2
    return jnp.concatenate([rows[:, :half], rows[:, half:]], axis=0)


def from_block(block):
    rows = block.shape[0] // 2
    return jnp.concatenate([block[:rows], block[rows:]], axis=1)


def swap_halves(left, right):
    top = lax.broadcasted_iota(jnp.int32, left.shape, 1) < 4
    return (
        jnp.where(top, left, pltpu.roll(right, 4, 1)),
        jnp.where(top, pltpu.roll(left, 4, 1), right),
    )


def load_blocks(ref, at, half):
    blocks = ref[:, :, at : at + half]
    pairs = blocks.reshape(blocks.shape[0] // 2, 2, 8, half)
    left, right = swap_halves(pairs[:, 0], pairs[:, 1])
    whole = jnp.concatenate([left, right], axis=2)
    return whole.reshape(whole.shape[0] * 8, 2 * half)


def call(body, out, grid=None, ins=None, outs=None, scratch=(), flops=0, moved=0, limit=12, name=None):
    kwargs = {}
    if grid is not None:
        kwargs["grid"] = grid
    if ins is not None:
        kwargs.update(in_specs=ins, out_specs=outs)
    return pl.pallas_call(
        body,
        out_shape=out,
        scratch_shapes=list(scratch),
        compiler_params=pltpu.CompilerParams(vmem_limit_bytes=limit * MIB),
        cost_estimate=pl.CostEstimate(flops=flops, bytes_accessed=moved, transcendentals=0),
        name=name,
        **kwargs,
    )


here = pl.BlockSpec(memory_space=pltpu.VMEM)
there = pl.BlockSpec(memory_space=pl.ANY)


def struct(*shape, dtype=f32):
    return jax.ShapeDtypeStruct(shape, dtype)


def flat(ref):
    return jnp.concatenate([ref[0], ref[1]], axis=0)


def spread_first(tok_ref, gain_ref, out_ref):
    x = flat(tok_ref)
    n = x * lax.rsqrt(mean(x * x) + eps) * gain_ref[...]
    out_ref[...] = jnp.broadcast_to(to_block(n), out_ref.shape)


def spread(row_ref, out_ref):
    out_ref[...] = jnp.broadcast_to(to_block(row_ref[...]), out_ref.shape)


def spread_last(row_ref, gain_ref, out_ref):
    width = gain_ref.shape[1]
    x = row_ref[:, :width]
    dx = row_ref[:, width:]
    r = lax.rsqrt(mean(x * x) + eps)
    n = x * r * gain_ref[...]
    dn = gain_ref[...] * (dx * r - x * r**3 * mean(x * dx))
    half = width // 2
    out_ref[:, :, :half] = jnp.broadcast_to(to_block(n), (out_ref.shape[0], 8, half))
    out_ref[:, :, half:] = jnp.broadcast_to(to_block(dn), (out_ref.shape[0], 8, half))


def sum_first(blocks_ref, tok_ref, out_ref):
    total = jnp.sum(blocks_ref[...], axis=0)
    half = total.shape[1] // 2
    width = tok_ref.shape[2]
    out_ref[:, :width] = flat(tok_ref) + from_block(total[:, :half])
    out_ref[:, width:] = from_block(total[:, half:])


def sum_last(blocks_ref, row_ref, curv_ref, rows_ref, out_ref):
    width = curv_ref.shape[2]
    g = flat(curv_ref) * (row_ref[:, width:] + from_block(jnp.sum(blocks_ref[...], axis=0)))
    rows_ref[...] = g
    out_ref[...] = jnp.broadcast_to(to_block(g), out_ref.shape)


def sum_back(blocks_ref, g_ref, row_ref, gain_ref, out_ref):
    width = gain_ref.shape[1]
    u = gain_ref[...] * from_block(jnp.sum(blocks_ref[...], axis=0))
    x = row_ref[:, :width]
    r = lax.rsqrt(mean(x * x) + eps)
    out_ref[...] = g_ref[...] + u * r - x * r**3 * mean(x * u)


def split(*refs):
    half = len(refs) // 2
    for in_ref, out_ref in zip(refs[:half], refs[half:]):
        keep_parts(out_ref, in_ref[...])


def run_split(*weights):
    rows, columns = weights[0].shape
    step = 256
    count = len(weights)
    return call(
        split,
        (struct(*tiled(rows, columns), dtype=bf16),) * count,
        grid=(rows // step,),
        ins=[pl.BlockSpec((step, columns), lambda j: (j, 0))] * count,
        outs=(pl.BlockSpec(tiled(step, columns), lambda j: (0, 0, j, 0)),) * count,
        flops=COVER_FLOPS,
        moved=8 * rows * columns * count,
        limit=26,
        name="split",
    )(*weights)


def turn(n_ref, a_ref, nt_ref, at_ref):
    for ref, turned in ((n_ref, nt_ref), (a_ref, at_ref)):
        for b in range(ref.shape[1]):
            for k in range(2):
                t = ref[k, b].T
                for c in range(turned.shape[1]):
                    turned[k, c, b * LANES : (b + 1) * LANES, :] = t[:, c * LANES : (c + 1) * LANES]


def run_turn(n, a):
    return call(
        turn,
        tuple(struct(*tiled(v.shape[1] * LANES, v.shape[2]), dtype=bf16) for v in (n, a)),
        flops=COVER_FLOPS,
        moved=4 * (n.size + a.size),
        limit=12,
        name="turn",
    )(n, a)


def tiled(rows, columns):
    return 2, columns // LANES, rows, LANES


def groups(ref, columns):
    first, last = (0, ref.shape[1] * LANES) if columns is None else (columns.start, columns.stop)
    return slice(first // LANES, last // LANES)


def cut(ref, rows=slice(None), columns=None):
    some = groups(ref, columns)
    return tuple(
        jnp.concatenate([ref[k, b, rows, :] for b in range(some.start, some.stop)], axis=1) for k in range(2)
    )


def keep_parts(ref, value, rows=slice(None), columns=None):
    some = groups(ref, columns)
    for k, part in enumerate(parts(value)):
        for at, b in enumerate(range(some.start, some.stop)):
            ref[k, b, rows, :] = part[:, at * LANES : (at + 1) * LANES]


def blocks_of(size):
    return [slice(at, at + UNITS) for at in range(0, size, UNITS)]


def output_columns(width):
    half = width // 2
    return [(at, slice(at, at + UNITS), slice(half + at, half + at + UNITS)) for at in range(0, half, UNITS)]


def store_pair(out_ref, at, left, right):
    rows, lanes = left.shape
    even, odd = swap_halves(left.reshape(rows // 8, 8, lanes), right.reshape(rows // 8, 8, lanes))
    out_ref[:, :, at : at + lanes] = jnp.stack([even, odd], axis=1).reshape(rows // 4, 8, lanes)


class Copies:
    def __init__(self, sems, sets=()):
        self.sems = sems
        self.count = 0
        self.sets = list(sets)
        self.begun = []

    def start(self, source, target):
        copy = pltpu.make_async_copy(source, target, self.sems.at[self.count])
        self.count += 1
        copy.start()
        return copy

    def begin(self, upto):
        for pairs in self.sets[len(self.begun) : upto]:
            self.begun.append([self.start(*pair) for pair in pairs])

    def wait(self, first, last):
        self.begin(last)
        for begun in self.begun[first:last]:
            wait(*begun)


def wait(*copies):
    for copy in copies:
        copy.wait()


def forward(last, blocks_ref, wi_hbm, vi_hbm, wo_hbm, vo_hbm, out_ref, n_hbm, a_hbm, p_hbm, *scratch):
    wi, vi, wo, vo, n, a, p, da, d, sems = scratch
    width, units = wi.shape[2], p.shape[1]
    half = width // 2

    def pair(first, second, cols):
        return [(source.at[:, groups(source, cols)], target.at[:, groups(target, cols)]) for source, target in (first, second)]

    inward = [pair((wi_hbm, wi), (vi_hbm, vi), c) for c in blocks_of(units)]
    outward = [
        pair((wo_hbm, wo), (vo_hbm, vo), c) for _, *both in output_columns(width) for c in both
    ]
    copies = Copies(sems, inward + outward)
    copies.begin(GROUP)
    keep_parts(n, load_blocks(blocks_ref, 0, half))
    copies.begin(2 * GROUP)
    if last:
        keep_parts(d, load_blocks(blocks_ref, half, half))
    for k, cols in enumerate(blocks_of(units)):
        if k % GROUP == 0:
            copies.wait(k, k + GROUP)
            copies.begin(k + 3 * GROUP)
        h = dot3(cut(n), cut(wi, columns=cols))
        dh = dot3(cut(n), cut(vi, columns=cols))
        if last:
            dh = dh + dot3(cut(d), cut(wi, columns=cols))
        act, slope = gelu_pair(h)
        p[:, cols] = slope
        keep_parts(a, act, columns=cols)
        keep_parts(da, slope * dh, columns=cols)
    results = [copies.start(n, n_hbm), copies.start(a, a_hbm), copies.start(p, p_hbm)]
    copies.wait(len(inward), len(copies.sets))
    for at, left, right in output_columns(width):
        if not last:
            store_pair(out_ref, at, *(dot3(cut(a), cut(wo, columns=c)) for c in (left, right)))
        terms = [
            dot3(cut(da), cut(wo, columns=c)) + dot3(cut(a), cut(vo, columns=c)) for c in (left, right)
        ]
        store_pair(out_ref, at + (0 if last else half), *terms)
    wait(*results)


def run_forward(blocks, weights, last):
    chips, _, lanes = blocks.shape
    width, units = weights[0].shape[2], weights[2].shape[2]
    rows = chips * 4
    out_lanes = (1 if last else 2) * width // 2
    inward = pltpu.VMEM(tiled(width, units), bf16)
    outward = pltpu.VMEM(tiled(units, width), bf16)
    small = pltpu.VMEM(tiled(rows, width), bf16)
    wide = pltpu.VMEM(tiled(rows, units), bf16)
    copies = 2 * (units // UNITS) + 2 * (width // UNITS) + 3
    return call(
        functools.partial(forward, last),
        (
            struct(chips, 8, out_lanes),
            struct(*tiled(rows, width), dtype=bf16),
            struct(*tiled(rows, units), dtype=bf16),
            struct(rows, units),
        ),
        ins=[here] + [there] * 4,
        outs=(here,) + (there,) * 3,
        scratch=[inward, inward, outward, outward, small, wide, pltpu.VMEM((rows, units), f32), wide]
        + [small if last else pltpu.VMEM((8, 128), bf16), pltpu.SemaphoreType.DMA((copies,))],
        flops=2 * rows * width * units * 5 * 3,
        moved=4 * width * units * 4,
        limit=40,
        name="forward_last" if last else "forward_first",
    )(blocks, *weights)


def backward(blocks_ref, p_hbm, wo_hbm, wi_hbm, out_ref, p, wo, wi, g, e, sems):
    units, width = wo.shape[2], wi.shape[2]
    first = [
        [(wo_hbm.at[:, :, c, :], wo.at[:, :, c, :]), (p_hbm.at[:, c], p.at[:, c])] for c in blocks_of(units)
    ]
    second = [
        [(wi_hbm.at[:, :, c, :], wi.at[:, :, c, :]) for c in (left, right)]
        for _, left, right in output_columns(width)
    ]
    copies = Copies(sems, first + second)
    copies.begin(len(first))
    keep_parts(g, load_blocks(blocks_ref, 0, width // 2))
    copies.wait(0, len(first))
    copies.begin(len(copies.sets))
    for c in blocks_of(units):
        keep_parts(e, p[:, c] * dot3(cut(g), cut(wo, rows=c), 1, 1), columns=c)
    copies.wait(len(first), len(copies.sets))
    for at, left, right in output_columns(width):
        store_pair(out_ref, at, *(dot3(cut(e), cut(wi, rows=c), 1, 1) for c in (left, right)))


def run_backward(blocks, p, wo, wi):
    chips, _, lanes = blocks.shape
    units, width = wo.shape[2], wi.shape[2]
    rows = chips * 4
    return call(
        backward,
        struct(chips, 8, lanes),
        ins=[here] + [there] * 3,
        outs=here,
        scratch=[
            pltpu.VMEM((rows, units), f32),
            pltpu.VMEM(tiled(units, width), bf16),
            pltpu.VMEM(tiled(width, units), bf16),
            pltpu.VMEM(tiled(rows, width), bf16),
            pltpu.VMEM(tiled(rows, units), bf16),
            pltpu.SemaphoreType.DMA((2 * (units // UNITS) + width // UNITS,)),
        ],
        flops=2 * rows * width * units * 6,
        moved=8 * width * units,
        limit=24,
        name="backward_last",
    )(blocks, p, wo, wi)


def finish(blocks_ref, p_hbm, wo_hbm, at_hbm, nt_hbm, in_hbm, out_hbm, *scratch):
    p, wo, at, nt, g, e, of_in, of_out, sems = scratch
    units, width = p.shape[1], nt.shape[2]
    sets = [[(at_hbm, at)], [(wo_hbm, wo), (p_hbm, p)], [(nt_hbm, nt)]]
    copies = Copies(sems, sets)
    copies.begin(2)
    keep_parts(g, load_blocks(blocks_ref, 0, width // 2))
    results = []

    def put(source, target, rows):
        step = UNITS // PIECES
        for first in range(rows.start, rows.stop, step):
            some = slice(first, first + step)
            results.append(copies.start(source.at[some, :], target.at[some, :]))

    copies.wait(0, 1)
    copies.begin(3)
    for c in blocks_of(units):
        of_out[c, :] = dot3(cut(at, rows=c), cut(g))
        put(of_out, out_hbm, c)
    copies.wait(1, 3)
    for c in blocks_of(units):
        keep_parts(e, p[:, c] * dot3(cut(g), cut(wo, rows=c), 1, 1), columns=c)
    for c in blocks_of(width):
        of_in[c, :] = dot3(cut(nt, rows=c), cut(e))
        put(of_in, in_hbm, c)
    wait(*results)


def run_finish(blocks, p, wo, at, nt):
    units, width = at.shape[2], nt.shape[2]
    rows = at.shape[1] * LANES
    return call(
        finish,
        (struct(width, units), struct(units, width)),
        ins=[here] + [there] * 4,
        outs=(there, there),
        scratch=[
            pltpu.VMEM((rows, units), f32),
            pltpu.VMEM(tiled(units, width), bf16),
            pltpu.VMEM(tiled(units, rows), bf16),
            pltpu.VMEM(tiled(width, rows), bf16),
            pltpu.VMEM(tiled(rows, width), bf16),
            pltpu.VMEM(tiled(rows, units), bf16),
            pltpu.VMEM((width, units), f32),
            pltpu.VMEM((units, width), f32),
            pltpu.SemaphoreType.DMA((4 + PIECES * (units + width) // UNITS,)),
        ],
        flops=2 * rows * width * units * 9,
        moved=12 * width * units,
        limit=36,
        name="finish",
    )(blocks, p, wo, at, nt)


def exchanged(blocks):
    return lax.all_to_all(blocks, "mp", 0, 0, tiled=True)


def on_device(tokens, curvature, gains, w_in, w_out, v_in, v_out):
    first = lax.axis_index("segment") == 0
    gain = gains
    weights = w_in[0], v_in[0], w_out[0], v_out[0]
    width = tokens.shape[2]
    rows = tokens.shape[0] * tokens.shape[1]
    chips = lax.axis_size("mp")
    total = rows * chips
    units = w_in.shape[2]
    single = struct(chips, 8, width // 2)
    double = struct(chips, 8, width)

    def blank(*shape, dtype=f32):
        return jnp.zeros(shape, dtype)

    def forward_first():
        blocks = exchanged(call(spread_first, single, name="spread_first")(tokens, gain))
        split_weights = run_split(*weights)
        out, n, a, p = run_forward(blocks, split_weights, False)
        both = call(sum_first, struct(rows, 2 * width), name="sum_first")(exchanged(out), tokens)
        return both, n, a, p, split_weights

    def no_forward():
        return (
            blank(rows, 2 * width),
            blank(*tiled(total, width), dtype=bf16),
            blank(*tiled(total, units), dtype=bf16),
            blank(total, units),
            run_split(*weights),
        )

    both, n0, a0, p0, split_weights = lax.cond(first, forward_first, no_forward)
    both = lax.ppermute(both, "segment", [(0, 1)])

    def layer_last(both, n0, a0, p0, split_weights):
        blocks = exchanged(call(spread_last, double, name="spread_last")(both, gain))
        out, n, a, p = run_forward(blocks, split_weights, True)
        g, blocks = call(sum_last, (struct(rows, width), single), name="sum_last")(
            exchanged(out), both, curvature
        )
        blocks = exchanged(blocks)
        out = run_backward(blocks, p, split_weights[2], split_weights[0])
        back = call(sum_back, struct(rows, width), name="sum_back")(exchanged(out), g, both, gain)
        return back, blocks, p, *run_turn(n, a)

    def keep(both, n0, a0, p0, split_weights):
        return blank(rows, width), blank(*single.shape), p0, *run_turn(n0, a0)

    back, blocks, p, nt, at = lax.cond(first, keep, layer_last, both, n0, a0, p0, split_weights)
    back = lax.ppermute(back, "segment", [(1, 0)])

    def cotangent_first(back, blocks):
        return exchanged(call(spread, single, name="spread")(back))

    def pass_on(back, blocks):
        return blocks

    blocks = lax.cond(first, cotangent_first, pass_on, back, blocks)

    product_in, product_out = run_finish(blocks, p, split_weights[2], at, nt)
    return product_in[None], product_out[None]


def solution(mesh):
    rows = P(None, "mp", None)
    layer_in = P("segment", None, "mp")
    layer_out = P("segment", "mp", None)
    return jax.shard_map(
        on_device,
        mesh=mesh,
        in_specs=(rows, rows, P("segment", None), layer_in, layer_out, layer_in, layer_out),
        out_specs=(layer_in, layer_out),
        check_vma=False,
    )
```

time: 211 us -> 201 us (0.953)
  blocking collectives: 68.8 us -> 46.6 us
  starting transfers between devices: 2.57 us -> 14.1 us
  Pallas kernels: 28.1 us -> 38.6 us
  waiting for transfers between devices: 108 us -> 98.8 us
    all_to_all x3 -> x2, blocking collectives: 68.8 us -> 46.6 us  [exchanged(): return lax.all_to_all(blocks, 'mp', 0, 0, tiled=True)]
    pallas_call x4 -> x5, Pallas kernels: 13.5 us -> 25.8 us  [the longest x1 12 us: run_split(): call(split, (struct(*tiled(rows, columns), dtype=bf16),) * count, grid=(r...]
    all_to_all x0 -> x1, starting transfers between devices: none -> 11.5 us  [exchanged(): return lax.all_to_all(blocks, 'mp', 0, 0, tiled=True)]
    ppermute x1, waiting for transfers between devices: 107 us -> 95.6 us  [on_device(): back = lax.ppermute(back, 'segment', [(1, 0)])]
    all_to_all x0 -> x1, waiting for transfers between devices: none -> 2.37 us  [exchanged(): return lax.all_to_all(blocks, 'mp', 0, 0, tiled=True)]
  transfers between devices with their start and end apart: 2 -> 3, of which waited for: 2 -> 3; matrix products, arithmetic and copies ran while one was open for 0% -> 0% of each run, Pallas kernels for 0% -> 6%
where the time goes in v1:
time: 201 us; the launch traced here: 200 us
  waiting for transfers between devices  98.8 us (49%)
  blocking collectives  46.6 us (23%)
  Pallas kernels  38.6 us (19%)
  starting transfers between devices  14.1 us (7%)
    ppermute x1, waiting for transfers between devices, on_device(): back = lax.ppermute(back, 'segment', [(1, 0)])  95.6 us
    all_to_all x2, blocking collectives, exchanged(): return lax.all_to_all(blocks, 'mp', 0, 0, tiled=True)  46.6 us
    pallas_call x1, Pallas kernels, run_forward(): call(functools.partial(forward, last), (struct(chips, 8, out_lanes), stru...  12.7 us
    pallas_call x1, Pallas kernels, run_split(): call(split, (struct(*tiled(rows, columns), dtype=bf16),) * count, grid=(r...  12 us
    all_to_all x1, starting transfers between devices, exchanged(): return lax.all_to_all(blocks, 'mp', 0, 0, tiled=True)  11.5 us
    pallas_call x1, Pallas kernels, run_finish(): call(finish, (struct(width, units), struct(units, width)), ins=[here] + [...  10.1 us
  transfers between devices with their start and end apart: 3, of which 3 were waited for; matrix products, arithmetic and copies ran while one was open for 0% of the time, Pallas kernels for 6%

profile of v1, /device:TPU:0, one launch (start us, length us, event | category | flops | bytes accessed | tf_op | source)
XLA Modules:
  0.0 200.2 jit_solution(4904597093260777909)
XLA Ops:
  0.6 0.0 copy-start.3
  0.6 68.3 %conditional.3 = (f32[4,2048]{1,0:T(4,128)S(1)}, bf16[2,8,256,128]{3,2,1,0:T(8,128)(2,1)S(1)}, bf16[2,8,256,128]{3,2,1,0:T(8,128)(2,1)S(1)}, f32[256,1024]{1,0:T...) conditional(s32[]{:T(128)} %convert_element_type.2, ...), branch_computations={%region_0.0_spmd, %region_1.0_spmd} | conditional | flops 25232932864 | bytes 57737340 | solution.py:465
  0.7 2.0 spread_first.1
  2.6 11.5 %all-to-all-start = ((f32[64,8,512]{2,1,0:T(8,128)}), f32[64,8,512]{2,1,0:T(8,128)S(1)}, u32[]{:S(2)}, u32[]{:S(2)}) async-start(f32[64,8,512]{2,1,0:T(8,128)} %spread_first.1), calls=%async_computation | async-start | bytes 2097152 | tf_op jit(solution)/shard_map/cond/branch_1_fun/all_to_all | solution.py:431
  14.2 12.0 %split.3 = (bf16[2,8,1024,128]{3,2,1,0:T(8,128)(2,1)}, bf16[2,8,1024,128]{3,2,1,0:T(8,128)(2,1)}, bf16[2,8,1024,128]{3,2,1,0:T(8,128)(2,1)}, bf16[2,8,1024,128]{3,2,1,0:T(8,128)(2,1)}) custom-call(f32[1024,1024]{1,0:T(8,128)} %get-tuple-element.56.refs_0_, f32[1024,1024]{1,0:T(8,128)} %get-tuple-element.57.refs_1_, f32[1024,1024]{1,0:T(8,128)} %get-tuple-element.58.refs_2_, ...), custom_call_target="tpu_custom_call" | custom-call | flops 17179869184 | bytes 33554432 | tf_op jit(solution)/shard_map/cond/branch_1_fun/split/pallas_call | solution.py:160
  26.1 2.4 %all-to-all-done.blocks_ref = f32[64,8,512]{2,1,0:T(8,128)S(1)} async-done(((f32[64,8,512]{2,1,0:T(8,128)}), f32[64,8,512]{2,1,0:T(8,128)S(1)}, u32[]{:S(2)}, u32[]{:S(2)}) %all-to-all-start) | async-done | bytes 1048608 | tf_op jit(solution)/shard_map/cond/branch_1_fun/all_to_all | solution.py:431
  28.5 12.7 %forward_first.1 = (f32[64,8,1024]{2,1,0:T(8,128)S(1)}, bf16[2,8,256,128]{3,2,1,0:T(8,128)(2,1)S(1)}, bf16[2,8,256,128]{3,2,1,0:T(8,128)(2,1)S(1)}, f32[256,1024]{1,0:T(8,128)}) custom-call(f32[64,8,512]{2,1,0:T(8,128)S(1)} %all-to-all-done.blocks_ref, bf16[2,8,1024,128]{3,2,1,0:T(8,128)(2,1)} %get-tuple-element.136.wi_hbm, ...), custom_call_target="tpu_custom_call" | custom-call | flops 8053063680 | bytes 16777216 | tf_op jit(solution)/shard_map/cond/branch_1_fun/forward_first/pallas_call | solution.py:311
  41.2 0.0 copy-start.1
  41.2 27.6 %all_to_all.28.blocks_ref = f32[64,8,1024]{2,1,0:T(8,128)S(1)} all-to-all(f32[64,8,1024]{2,1,0:T(8,128)S(1)} %get-tuple-element.64), channel_id=1, replica_groups=mesh['segment'=2,'mp'=64] {'mp'}, dimensions={0} | all-to-all | bytes 4194304 | tf_op jit(solution)/shard_map/cond/branch_1_fun/all_to_all | solution.py:431
  68.8 0.0 copy-done.1
  68.8 0.1 sum_first.1
  69.0 1.3 collective-permute-start
  70.3 0.8 collective-permute-done
  71.1 0.0 copy-done.3
  71.1 2.9 %conditional.4 = (f32[4,1024]{1,0:T(4,128)S(1)}, f32[256,1024]{1,0:T(8,128)}, bf16[2,2,1024,128]{3,2,1,0:T(8,128)(2,1)}, bf16[2,2,1024,128]{3,2,1,0:T(8,128)(2,1)}, f32[64,8,512]{2,1,0:T(8,128)}) conditional(s32[]{:T(128)} %convert_element_type.2, (f32[4,2048]{1,0:T(4,128)S(1)}, f32[1,1024]{1,0:T(1,128)}, bf16[2,8,1024,128]{3,2,1,0:T(8,128)(2,1)}, ...), branch_computations={%region_2.0_spmd, %region_3.0_spmd} | conditional | flops 28454158336 | bytes 61882524 | solution.py:482
  71.1 1.6 turn.3
  72.7 1.2 broadcast.14
  74.0 1.3 collective-permute-start.1
  75.2 95.6 %collective-permute-done.1 = f32[4,1024]{1,0:T(4,128)S(1)} collective-permute-done((f32[4,1024]{1,0:T(4,128)S(1)}, f32[4,1024]{1,0:T(4,128)S(1)}, u32[]{:S(2)}, u32[]{:S(2)}) %collective-permute-start.1) | collective-permute-done | bytes 16416 | tf_op jit(solution)/shard_map/ppermute | solution.py:483
  170.9 19.1 %conditional.5 = (f32[64,8,512]{2,1,0:T(8,128)}) conditional(s32[]{:T(128)} %convert_element_type.2, f32[64,8,512]{2,1,0:T(8,128)} %get-tuple-element.113, f32[4,1024]{1,0:T(4,128)S(1)} %collective-permute-done.1), branch_computations={%region_4.0_spmd, %region_5.0_spmd} | conditional | bytes 2097160 | solution.py:491
  170.9 0.1 spread.1
  171.0 18.9 %all_to_all.32 = f32[64,8,512]{2,1,0:T(8,128)} all-to-all(f32[64,8,512]{2,1,0:T(8,128)S(1)} %spread.1), channel_id=1, replica_groups=mesh['segment'=2,'mp'=64] {'mp'}, dimensions={0} | all-to-all | bytes 2097152 | tf_op jit(solution)/shard_map/cond/branch_1_fun/all_to_all | solution.py:431
  189.9 10.1 %finish.1 = (f32[1024,1024]{1,0:T(8,128)}, f32[1024,1024]{1,0:T(8,128)}) custom-call(f32[64,8,512]{2,1,0:T(8,128)} %get-tuple-element.150.blocks_ref, f32[256,1024]{1,0:T(8,128)} %get-tuple-element.115.p_hbm, bf16[2,8,1024,128]{3,2,1,0:T(8,128)(2,1)} %get-tuple-element.108.wo_hbm, bf16[2,2,1024,128]{3,2,1,0:T(8,128)(2,1)} %get-tuple-element.116.at_hbm, ...), custom_call_target="tpu_custom_call" | custom-call | flops 4831838208 | bytes 12582912 | tf_op jit(solution)/shard_map/finish/pallas_call | solution.py:407
  (1 shorter events, 0.0 us)
Async XLA Ops:
  0.6 70.5 %copy-start.3 = (f32[2,2,1024]{2,1,0:T(2,128)S(1)}, f32[2,2,1024]{2,1,0:T(2,128)}, u32[]{:S(2)}) copy-start(f32[2,2,1024]{2,1,0:T(2,128)} %param.14) | copy-start | bytes 49156
  2.6 25.9 %all-to-all-start = ((f32[64,8,512]{2,1,0:T(8,128)}), f32[64,8,512]{2,1,0:T(8,128)S(1)}, u32[]{:S(2)}, u32[]{:S(2)}) async-start(f32[64,8,512]{2,1,0:T(8,128)} %spread_first.1), calls=%async_computation | async-start | bytes 2097152 | tf_op jit(solution)/shard_map/cond/branch_1_fun/all_to_all | solution.py:431
  41.2 27.6 %copy-start.1 = (f32[2,2,1024]{2,1,0:T(2,128)S(1)}, f32[2,2,1024]{2,1,0:T(2,128)}, u32[]{:S(2)}) copy-start(f32[2,2,1024]{2,1,0:T(2,128)} %get-tuple-element.121.tok_ref) | copy-start | bytes 49156 | tf_op jit(solution)/shard_map/cond
  69.0 2.1 %collective-permute-start = (f32[4,2048]{1,0:T(4,128)S(1)}, f32[4,2048]{1,0:T(4,128)S(1)}, u32[]{:S(2)}, u32[]{:S(2)}) collective-permute-start(f32[4,2048]{1,0:T(4,128)S(1)} %get-tuple-element.105), channel_id=1, source_target_pairs={{0,64},{1,65},{2,66},{3,67},{4,68},{5,69},{6,70},{7,71},{8,72},{9,... | collective-permute-start | bytes 98312 | tf_op jit(solution)/shard_map/ppermute | solution.py:466
  74.0 96.9 %collective-permute-start.1 = (f32[4,1024]{1,0:T(4,128)S(1)}, f32[4,1024]{1,0:T(4,128)S(1)}, u32[]{:S(2)}, u32[]{:S(2)}) collective-permute-start(f32[4,1024]{1,0:T(4,128)S(1)} %get-tuple-element.114), channel_id=1, source_target_pairs={{64,0},{65,1},{66,2},{67,3},{68,4},{69,5},{70,6},{71,7},{72,8},{73... | collective-permute-start | bytes 49160 | tf_op jit(solution)/shard_map/ppermute | solution.py:483

commit v2 on v1

--- a/solution.py
+++ b/solution.py
@@ -258,11 +258,16 @@
 
 def forward(last, blocks_ref, wi_hbm, vi_hbm, wo_hbm, vo_hbm, out_ref, n_hbm, a_hbm, p_hbm, *scratch):
     wi, vi, wo, vo, n, a, p, da, d, sems = scratch
-    width, units = wi.shape[2], p.shape[1]
+    units, width = wo.shape
     half = width // 2
 
     def pair(first, second, cols):
-        return [(source.at[:, groups(source, cols)], target.at[:, groups(target, cols)]) for source, target in (first, second)]
+        if len(first[0].shape) == 2:
+            return [(source.at[:, cols], target.at[:, cols]) for source, target in (first, second)]
+        return [
+            (source.at[:, groups(source, cols)], target.at[:, groups(target, cols)])
+            for source, target in (first, second)
+        ]
 
     inward = [pair((wi_hbm, wi), (vi_hbm, vi), c) for c in blocks_of(units)]
     outward = [
@@ -271,7 +276,6 @@
     copies = Copies(sems, inward + outward)
     copies.begin(GROUP)
     keep_parts(n, load_blocks(blocks_ref, 0, half))
-    copies.begin(2 * GROUP)
     if last:
         keep_parts(d, load_blocks(blocks_ref, half, half))
     for k, cols in enumerate(blocks_of(units)):
@@ -289,10 +293,11 @@
     results = [copies.start(n, n_hbm), copies.start(a, a_hbm), copies.start(p, p_hbm)]
     copies.wait(len(inward), len(copies.sets))
     for at, left, right in output_columns(width):
+        wo_here = [parts(wo[:, c]) for c in (left, right)]
         if not last:
-            store_pair(out_ref, at, *(dot3(cut(a), cut(wo, columns=c)) for c in (left, right)))
+            store_pair(out_ref, at, *(dot3(cut(a), w) for w in wo_here))
         terms = [
-            dot3(cut(da), cut(wo, columns=c)) + dot3(cut(a), cut(vo, columns=c)) for c in (left, right)
+            dot3(cut(da), w) + dot3(cut(a), parts(vo[:, c])) for w, c in zip(wo_here, (left, right))
         ]
         store_pair(out_ref, at + (0 if last else half), *terms)
     wait(*results)
@@ -300,11 +305,11 @@
 
 def run_forward(blocks, weights, last):
     chips, _, lanes = blocks.shape
-    width, units = weights[0].shape[2], weights[2].shape[2]
+    units, width = weights[2].shape
     rows = chips * 4
     out_lanes = (1 if last else 2) * width // 2
     inward = pltpu.VMEM(tiled(width, units), bf16)
-    outward = pltpu.VMEM(tiled(units, width), bf16)
+    outward = pltpu.VMEM((units, width), f32)
     small = pltpu.VMEM(tiled(rows, width), bf16)
     wide = pltpu.VMEM(tiled(rows, units), bf16)
     copies = 2 * (units // UNITS) + 2 * (width // UNITS) + 3
@@ -327,58 +332,53 @@
     )(blocks, *weights)
 
 
-def backward(blocks_ref, p_hbm, wo_hbm, wi_hbm, out_ref, p, wo, wi, g, e, sems):
-    units, width = wo.shape[2], wi.shape[2]
-    first = [
-        [(wo_hbm.at[:, :, c, :], wo.at[:, :, c, :]), (p_hbm.at[:, c], p.at[:, c])] for c in blocks_of(units)
-    ]
-    second = [
-        [(wi_hbm.at[:, :, c, :], wi.at[:, :, c, :]) for c in (left, right)]
-        for _, left, right in output_columns(width)
-    ]
-    copies = Copies(sems, first + second)
-    copies.begin(len(first))
+def backward(blocks_ref, p_hbm, wo, wi, out_ref, blocks_hbm, p, g, e, sems):
+    units, width = wo.shape
+    copies = Copies(sems)
+    slopes = copies.start(p_hbm, p)
+    handed = copies.start(blocks_ref, blocks_hbm)
     keep_parts(g, load_blocks(blocks_ref, 0, width // 2))
-    copies.wait(0, len(first))
-    copies.begin(len(copies.sets))
-    for c in blocks_of(units):
-        keep_parts(e, p[:, c] * dot3(cut(g), cut(wo, rows=c), 1, 1), columns=c)
-    copies.wait(len(first), len(copies.sets))
+    for k, c in enumerate(blocks_of(units)):
+        back = dot3(cut(g), parts(wo[c, :]), 1, 1)
+        if k == 0:
+            wait(slopes)
+        keep_parts(e, p[:, c] * back, columns=c)
     for at, left, right in output_columns(width):
-        store_pair(out_ref, at, *(dot3(cut(e), cut(wi, rows=c), 1, 1) for c in (left, right)))
+        store_pair(out_ref, at, *(dot3(cut(e), parts(wi[c, :]), 1, 1) for c in (left, right)))
+    wait(handed)
 
 
 def run_backward(blocks, p, wo, wi):
     chips, _, lanes = blocks.shape
-    units, width = wo.shape[2], wi.shape[2]
+    units, width = wo.shape
     rows = chips * 4
     return call(
         backward,
-        struct(chips, 8, lanes),
-        ins=[here] + [there] * 3,
-        outs=here,
+        (struct(chips, 8, lanes), struct(chips, 8, lanes)),
+        ins=[here, there, here, here],
+        outs=(here, there),
         scratch=[
             pltpu.VMEM((rows, units), f32),
-            pltpu.VMEM(tiled(units, width), bf16),
-            pltpu.VMEM(tiled(width, units), bf16),
             pltpu.VMEM(tiled(rows, width), bf16),
             pltpu.VMEM(tiled(rows, units), bf16),
-            pltpu.SemaphoreType.DMA((2 * (units // UNITS) + width // UNITS,)),
+            pltpu.SemaphoreType.DMA((2,)),
         ],
         flops=2 * rows * width * units * 6,
         moved=8 * width * units,
-        limit=24,
+        limit=12,
         name="backward_last",
     )(blocks, p, wo, wi)
 
 
-def finish(blocks_ref, p_hbm, wo_hbm, at_hbm, nt_hbm, in_hbm, out_hbm, *scratch):
-    p, wo, at, nt, g, e, of_in, of_out, sems = scratch
+def finish(blocks_hbm, p_hbm, wo_hbm, at_hbm, nt_hbm, in_hbm, out_hbm, *scratch):
+    blocks, p, wo, at, nt, g, e, of_in, of_out, sems = scratch
     units, width = p.shape[1], nt.shape[2]
-    sets = [[(at_hbm, at)], [(wo_hbm, wo), (p_hbm, p)], [(nt_hbm, nt)]]
+    sets = [[(blocks_hbm, blocks)], [(at_hbm, at)], [(wo_hbm, wo), (p_hbm, p)], [(nt_hbm, nt)]]
     copies = Copies(sems, sets)
     copies.begin(2)
-    keep_parts(g, load_blocks(blocks_ref, 0, width // 2))
+    copies.wait(0, 1)
+    copies.begin(4)
+    keep_parts(g, load_blocks(blocks, 0, width // 2))
     results = []
 
     def put(source, target, rows):
@@ -387,14 +387,13 @@
             some = slice(first, first + step)
             results.append(copies.start(source.at[some, :], target.at[some, :]))
 
-    copies.wait(0, 1)
-    copies.begin(3)
+    copies.wait(1, 2)
     for c in blocks_of(units):
         of_out[c, :] = dot3(cut(at, rows=c), cut(g))
         put(of_out, out_hbm, c)
-    copies.wait(1, 3)
+    copies.wait(2, 4)
     for c in blocks_of(units):
-        keep_parts(e, p[:, c] * dot3(cut(g), cut(wo, rows=c), 1, 1), columns=c)
+        keep_parts(e, p[:, c] * dot3(cut(g), parts(wo[c, :]), 1, 1), columns=c)
     for c in blocks_of(width):
         of_in[c, :] = dot3(cut(nt, rows=c), cut(e))
         put(of_in, in_hbm, c)
@@ -407,18 +406,19 @@
     return call(
         finish,
         (struct(width, units), struct(units, width)),
-        ins=[here] + [there] * 4,
+        ins=[there] * 5,
         outs=(there, there),
         scratch=[
+            pltpu.VMEM(blocks.shape, f32),
             pltpu.VMEM((rows, units), f32),
-            pltpu.VMEM(tiled(units, width), bf16),
+            pltpu.VMEM((units, width), f32),
             pltpu.VMEM(tiled(units, rows), bf16),
             pltpu.VMEM(tiled(width, rows), bf16),
             pltpu.VMEM(tiled(rows, width), bf16),
             pltpu.VMEM(tiled(rows, units), bf16),
             pltpu.VMEM((width, units), f32),
             pltpu.VMEM((units, width), f32),
-            pltpu.SemaphoreType.DMA((4 + PIECES * (units + width) // UNITS,)),
+            pltpu.SemaphoreType.DMA((5 + PIECES * (units + width) // UNITS,)),
         ],
         flops=2 * rows * width * units * 9,
         moved=12 * width * units,
@@ -448,10 +448,10 @@
 
     def forward_first():
         blocks = exchanged(call(spread_first, single, name="spread_first")(tokens, gain))
-        split_weights = run_split(*weights)
-        out, n, a, p = run_forward(blocks, split_weights, False)
+        inward = run_split(*weights[:2])
+        out, n, a, p = run_forward(blocks, (*inward, *weights[2:]), False)
         both = call(sum_first, struct(rows, 2 * width), name="sum_first")(exchanged(out), tokens)
-        return both, n, a, p, split_weights
+        return both, n, a, p, inward
 
     def no_forward():
         return (
@@ -459,27 +459,26 @@
             blank(*tiled(total, width), dtype=bf16),
             blank(*tiled(total, units), dtype=bf16),
             blank(total, units),
-            run_split(*weights),
+            run_split(*weights[:2]),
         )
 
-    both, n0, a0, p0, split_weights = lax.cond(first, forward_first, no_forward)
+    both, n0, a0, p0, inward = lax.cond(first, forward_first, no_forward)
     both = lax.ppermute(both, "segment", [(0, 1)])
 
-    def layer_last(both, n0, a0, p0, split_weights):
+    def layer_last(both, n0, a0, p0, inward):
         blocks = exchanged(call(spread_last, double, name="spread_last")(both, gain))
-        out, n, a, p = run_forward(blocks, split_weights, True)
+        out, n, a, p = run_forward(blocks, (*inward, *weights[2:]), True)
         g, blocks = call(sum_last, (struct(rows, width), single), name="sum_last")(
             exchanged(out), both, curvature
         )
-        blocks = exchanged(blocks)
-        out = run_backward(blocks, p, split_weights[2], split_weights[0])
+        out, blocks = run_backward(exchanged(blocks), p, weights[2], weights[0])
         back = call(sum_back, struct(rows, width), name="sum_back")(exchanged(out), g, both, gain)
         return back, blocks, p, *run_turn(n, a)
 
-    def keep(both, n0, a0, p0, split_weights):
+    def keep(both, n0, a0, p0, inward):
         return blank(rows, width), blank(*single.shape), p0, *run_turn(n0, a0)
 
-    back, blocks, p, nt, at = lax.cond(first, keep, layer_last, both, n0, a0, p0, split_weights)
+    back, blocks, p, nt, at = lax.cond(first, keep, layer_last, both, n0, a0, p0, inward)
     back = lax.ppermute(back, "segment", [(1, 0)])
 
     def cotangent_first(back, blocks):
@@ -490,7 +489,7 @@
 
     blocks = lax.cond(first, cotangent_first, pass_on, back, blocks)
 
-    product_in, product_out = run_finish(blocks, p, split_weights[2], at, nt)
+    product_in, product_out = run_finish(blocks, p, weights[2], at, nt)
     return product_in[None], product_out[None]
 
 

time: 201 us -> 198 us (0.985)
  waiting for transfers between devices: 98.8 us -> 104 us
  Pallas kernels: 38.6 us -> 34.1 us
  blocking collectives: 46.6 us -> 43.3 us
    pallas_call x1, Pallas kernels: 12 us -> 7.34 us  [run_split(): call(split, (struct(*tiled(rows, columns), dtype=bf16),) * count, grid=(r...]
    all_to_all x1, waiting for transfers between devices: 2.37 us -> 7 us  [exchanged(): return lax.all_to_all(blocks, 'mp', 0, 0, tiled=True)]
    all_to_all x2, blocking collectives: 46.6 us -> 43.3 us  [exchanged(): return lax.all_to_all(blocks, 'mp', 0, 0, tiled=True)]
  transfers between devices with their start and end apart: 3 -> 3, of which waited for: 3 -> 3; matrix products, arithmetic and copies ran while one was open for 0% -> 0% of each run, Pallas kernels for 6% -> 4%
where the time goes in v2:
time: 198 us; the launch traced here: 197 us
  waiting for transfers between devices  104 us (53%)
  blocking collectives  43.3 us (22%)
  Pallas kernels  34.1 us (17%)
  starting transfers between devices  14.1 us (7%)
    ppermute x1, waiting for transfers between devices, on_device(): back = lax.ppermute(back, 'segment', [(1, 0)])  96.1 us
    all_to_all x2, blocking collectives, exchanged(): return lax.all_to_all(blocks, 'mp', 0, 0, tiled=True)  43.3 us
    pallas_call x1, Pallas kernels, run_forward(): call(functools.partial(forward, last), (struct(chips, 8, out_lanes), stru...  12.7 us
    all_to_all x1, starting transfers between devices, exchanged(): return lax.all_to_all(blocks, 'mp', 0, 0, tiled=True)  11.5 us
    pallas_call x1, Pallas kernels, run_finish(): call(finish, (struct(width, units), struct(units, width)), ins=[there] *...  10.3 us
    pallas_call x1, Pallas kernels, run_split(): call(split, (struct(*tiled(rows, columns), dtype=bf16),) * count, grid=(r...  7.34 us
    all_to_all x1, waiting for transfers between devices, exchanged(): return lax.all_to_all(blocks, 'mp', 0, 0, tiled=True)  7 us
  transfers between devices with their start and end apart: 3, of which 3 were waited for; matrix products, arithmetic and copies ran while one was open for 0% of the time, Pallas kernels for 4%

profile of v2, /device:TPU:0, one launch (start us, length us, event | category | flops | bytes accessed | tf_op | source)
XLA Modules:
  0.0 197.3 jit_solution(8527325059784611700)
XLA Ops:
  0.6 0.0 copy-start.2
  0.6 65.0 %conditional.3 = (f32[4,2048]{1,0:T(4,128)S(1)}, bf16[2,8,256,128]{3,2,1,0:T(8,128)(2,1)S(1)}, bf16[2,8,256,128]{3,2,1,0:T(8,128)(2,1)S(1)}, f32[256,1024]{1,0:T...) conditional(s32[]{:T(128)} %convert_element_type.2, (f32[1024,1024]{1,0:T(8,128)}, ...), branch_computations={%region_0.0_spmd, %region_1.0_spmd} | conditional | flops 25232932864 | bytes 40960108 | solution.py:465
  0.7 1.9 spread_first.1
  2.6 11.5 %all-to-all-start = ((f32[64,8,512]{2,1,0:T(8,128)}), f32[64,8,512]{2,1,0:T(8,128)S(1)}, u32[]{:S(2)}, u32[]{:S(2)}) async-start(f32[64,8,512]{2,1,0:T(8,128)} %spread_first.1), calls=%async_computation | async-start | bytes 2097152 | tf_op jit(solution)/shard_map/cond/branch_1_fun/all_to_all | solution.py:431
  14.1 7.3 %split.3 = (bf16[2,8,1024,128]{3,2,1,0:T(8,128)(2,1)}, bf16[2,8,1024,128]{3,2,1,0:T(8,128)(2,1)}) custom-call(f32[1024,1024]{1,0:T(8,128)} %get-tuple-element.49.refs_0_, f32[1024,1024]{1,0:T(8,128)} %get-tuple-element.50.refs_1_), custom_call_target="tpu_custom_call" | custom-call | flops 17179869184 | bytes 16777216 | tf_op jit(solution)/shard_map/cond/branch_1_fun/split/pallas_call | solution.py:160
  21.4 7.0 %all-to-all-done.blocks_ref = f32[64,8,512]{2,1,0:T(8,128)S(1)} async-done(((f32[64,8,512]{2,1,0:T(8,128)}), f32[64,8,512]{2,1,0:T(8,128)S(1)}, u32[]{:S(2)}, u32[]{:S(2)}) %all-to-all-start) | async-done | bytes 1048608 | tf_op jit(solution)/shard_map/cond/branch_1_fun/all_to_all | solution.py:431
  28.4 12.7 %forward_first.1 = (f32[64,8,1024]{2,1,0:T(8,128)S(1)}, bf16[2,8,256,128]{3,2,1,0:T(8,128)(2,1)S(1)}, bf16[2,8,256,128]{3,2,1,0:T(8,128)(2,1)S(1)}, f32[256,1024]{1,0:T(8,128)}) custom-call(f32[64,8,512]{2,1,0:T(8,128)S(1)} %all-to-all-done.blocks_ref, bf16[2,8,1024,128]{3,2,1,0:T(8,128)(2,1)} %get-tuple-element.124.wi_hbm, ...), custom_call_target="tpu_custom_call" | custom-call | flops 8053063680 | bytes 16777216 | tf_op jit(solution)/shard_map/cond/branch_1_fun/forward_first/pallas_call | solution.py:316
  41.1 0.0 copy-start
  41.1 24.3 %all_to_all.28.blocks_ref = f32[64,8,1024]{2,1,0:T(8,128)S(1)} all-to-all(f32[64,8,1024]{2,1,0:T(8,128)S(1)} %get-tuple-element.55), channel_id=1, replica_groups=mesh['segment'=2,'mp'=64] {'mp'}, dimensions={0} | all-to-all | bytes 4194304 | tf_op jit(solution)/shard_map/cond/branch_1_fun/all_to_all | solution.py:431
  65.5 0.0 copy-done
  65.5 0.1 sum_first.1
  65.6 1.3 collective-permute-start
  66.9 0.8 collective-permute-done
  67.7 0.0 copy-done.2
  67.7 2.7 %conditional.4 = (f32[4,1024]{1,0:T(4,128)S(1)}, f32[64,8,512]{2,1,0:T(8,128)}, f32[256,1024]{1,0:T(8,128)}, bf16[2,2,1024,128]{3,2,1,0:T(8,128)(2,1)}, bf16[2,2,1024,128]{3,2,1,0:T(8,128)(2,1)}) conditional(s32[]{:T(128)} %convert_element_type.2, (f32[4,2048]{1,0:T(4,128)S(1)}, f32[1,1024]{1,0:T(1,128)}, bf16[2,8,1024,128]{3,2,1,0:T(8,128)(2,1)}, ...), branch_computations={%region_2.0_spmd, %region_3.0_spmd} | conditional | flops 28454158336 | bytes 91242688 | solution.py:481
  67.7 1.6 turn.3
  69.4 1.1 broadcast.14
  70.4 1.3 collective-permute-start.1
  71.7 96.1 %collective-permute-done.1 = f32[4,1024]{1,0:T(4,128)S(1)} collective-permute-done((f32[4,1024]{1,0:T(4,128)S(1)}, f32[4,1024]{1,0:T(4,128)S(1)}, u32[]{:S(2)}, u32[]{:S(2)}) %collective-permute-start.1) | collective-permute-done | bytes 16416 | tf_op jit(solution)/shard_map/ppermute | solution.py:482
  167.8 19.1 %conditional.5 = (f32[64,8,512]{2,1,0:T(8,128)}) conditional(s32[]{:T(128)} %convert_element_type.2, f32[64,8,512]{2,1,0:T(8,128)} %get-tuple-element.103, f32[4,1024]{1,0:T(4,128)S(1)} %collective-permute-done.1), branch_computations={%region_4.0_spmd, %region_5.0_spmd} | conditional | bytes 2097160 | solution.py:490
  167.8 0.1 spread.1
  167.9 18.9 %all_to_all.32 = f32[64,8,512]{2,1,0:T(8,128)} all-to-all(f32[64,8,512]{2,1,0:T(8,128)S(1)} %spread.1), channel_id=1, replica_groups=mesh['segment'=2,'mp'=64] {'mp'}, dimensions={0} | all-to-all | bytes 2097152 | tf_op jit(solution)/shard_map/cond/branch_1_fun/all_to_all | solution.py:431
  186.9 10.3 %finish.1 = (f32[1024,1024]{1,0:T(8,128)}, f32[1024,1024]{1,0:T(8,128)}) custom-call(f32[64,8,512]{2,1,0:T(8,128)} %get-tuple-element.136.blocks_hbm, f32[256,1024]{1,0:T(8,128)} %get-tuple-element.105.p_hbm, f32[1024,1024]{1,0:T(8,128)} %bitcast.15, bf16[2,2,1024,128]{3,2,1,0:T(8,128)(2,1)} %get-tuple-element.106.at_hbm, ...), custom_call_target="tpu_custom_call" | custom-call | flops 4831838208 | bytes 12582912 | tf_op jit(solution)/shard_map/finish/pallas_call | solution.py:406
  (1 shorter events, 0.0 us)
Async XLA Ops:
  0.6 67.1 %copy-start.2 = (f32[2,2,1024]{2,1,0:T(2,128)S(1)}, f32[2,2,1024]{2,1,0:T(2,128)}, u32[]{:S(2)}) copy-start(f32[2,2,1024]{2,1,0:T(2,128)} %param.14) | copy-start | bytes 49156
  2.6 25.9 %all-to-all-start = ((f32[64,8,512]{2,1,0:T(8,128)}), f32[64,8,512]{2,1,0:T(8,128)S(1)}, u32[]{:S(2)}, u32[]{:S(2)}) async-start(f32[64,8,512]{2,1,0:T(8,128)} %spread_first.1), calls=%async_computation | async-start | bytes 2097152 | tf_op jit(solution)/shard_map/cond/branch_1_fun/all_to_all | solution.py:431
  41.1 24.3 %copy-start = (f32[2,2,1024]{2,1,0:T(2,128)S(1)}, f32[2,2,1024]{2,1,0:T(2,128)}, u32[]{:S(2)}) copy-start(f32[2,2,1024]{2,1,0:T(2,128)} %get-tuple-element.111.tok_ref) | copy-start | bytes 49156 | tf_op jit(solution)/shard_map/cond
  65.6 2.1 %collective-permute-start = (f32[4,2048]{1,0:T(4,128)S(1)}, f32[4,2048]{1,0:T(4,128)S(1)}, u32[]{:S(2)}, u32[]{:S(2)}) collective-permute-start(f32[4,2048]{1,0:T(4,128)S(1)} %get-tuple-element.97), channel_id=1, source_target_pairs={{0,64},{1,65},{2,66},{3,67},{4,68},{5,69},{6,70},{7,71},{8,72},{9,... | collective-permute-start | bytes 98312 | tf_op jit(solution)/shard_map/ppermute | solution.py:466
  70.4 97.4 %collective-permute-start.1 = (f32[4,1024]{1,0:T(4,128)S(1)}, f32[4,1024]{1,0:T(4,128)S(1)}, u32[]{:S(2)}, u32[]{:S(2)}) collective-permute-start(f32[4,1024]{1,0:T(4,128)S(1)} %get-tuple-element.104), channel_id=1, source_target_pairs={{64,0},{65,1},{66,2},{67,3},{68,4},{69,5},{70,6},{71,7},{72,8},{73... | collective-permute-start | bytes 49160 | tf_op jit(solution)/shard_map/ppermute | solution.py:482

commit v3 on v2

--- a/solution.py
+++ b/solution.py
@@ -261,18 +261,18 @@
     units, width = wo.shape
     half = width // 2
 
-    def pair(first, second, cols):
-        if len(first[0].shape) == 2:
-            return [(source.at[:, cols], target.at[:, cols]) for source, target in (first, second)]
-        return [
-            (source.at[:, groups(source, cols)], target.at[:, groups(target, cols)])
-            for source, target in (first, second)
-        ]
-
-    inward = [pair((wi_hbm, wi), (vi_hbm, vi), c) for c in blocks_of(units)]
-    outward = [
-        pair((wo_hbm, wo), (vo_hbm, vo), c) for _, *both in output_columns(width) for c in both
-    ]
+    def some(source, target, cols):
+        if len(source.shape) == 2:
+            return source.at[:, cols], target.at[:, cols]
+        return source.at[:, groups(source, cols)], target.at[:, groups(target, cols)]
+
+    inward = [[some(wi_hbm, wi, c), some(vi_hbm, vi, c)] for c in blocks_of(units)]
+    outward = [[some(wo_hbm, wo, c)] for _, *both in output_columns(width) for c in both]
+    if last:
+        vo = vo_hbm
+    else:
+        for k, c in enumerate(c for _, *both in output_columns(width) for c in both):
+            outward[k].append(some(vo_hbm, vo, c))
     copies = Copies(sems, inward + outward)
     copies.begin(GROUP)
     keep_parts(n, load_blocks(blocks_ref, 0, half))
@@ -321,9 +321,9 @@
             struct(*tiled(rows, units), dtype=bf16),
             struct(rows, units),
         ),
-        ins=[here] + [there] * 4,
+        ins=[here] + [there] * 3 + [here if last else there],
         outs=(here,) + (there,) * 3,
-        scratch=[inward, inward, outward, outward, small, wide, pltpu.VMEM((rows, units), f32), wide]
+        scratch=[inward, inward, outward, pltpu.VMEM((8, 128), f32) if last else outward, small, wide, pltpu.VMEM((rows, units), f32), wide]
         + [small if last else pltpu.VMEM((8, 128), bf16), pltpu.SemaphoreType.DMA((copies,))],
         flops=2 * rows * width * units * 5 * 3,
         moved=4 * width * units * 4,

time: 198 us -> 197 us (level)
  no operation moved by 1% of the time
where the time goes in v3:
time: 197 us; the launch traced here: 196 us
  waiting for transfers between devices  103 us (52%)
  blocking collectives  43.3 us (22%)
  Pallas kernels  34.1 us (17%)
  starting transfers between devices  14.1 us (7%)
    ppermute x1, waiting for transfers between devices, on_device(): back = lax.ppermute(back, 'segment', [(1, 0)])  95 us
    all_to_all x2, blocking collectives, exchanged(): return lax.all_to_all(blocks, 'mp', 0, 0, tiled=True)  43.3 us
    pallas_call x1, Pallas kernels, run_forward(): call(functools.partial(forward, last), (struct(chips, 8, out_lanes), stru...  12.7 us
    all_to_all x1, starting transfers between devices, exchanged(): return lax.all_to_all(blocks, 'mp', 0, 0, tiled=True)  11.5 us
    pallas_call x1, Pallas kernels, run_finish(): call(finish, (struct(width, units), struct(units, width)), ins=[there] *...  10.3 us
    pallas_call x1, Pallas kernels, run_split(): call(split, (struct(*tiled(rows, columns), dtype=bf16),) * count, grid=(r...  7.34 us
    all_to_all x1, waiting for transfers between devices, exchanged(): return lax.all_to_all(blocks, 'mp', 0, 0, tiled=True)  7 us
  transfers between devices with their start and end apart: 3, of which 3 were waited for; matrix products, arithmetic and copies ran while one was open for 0% of the time, Pallas kernels for 4%

profile of v3, /device:TPU:0, one launch (start us, length us, event | category | flops | bytes accessed | tf_op | source)
XLA Modules:
  0.0 196.3 jit_solution(12677137485523595617)
XLA Ops:
  0.6 0.0 copy-start.2
  0.6 65.0 %conditional.3 = (f32[4,2048]{1,0:T(4,128)S(1)}, bf16[2,8,256,128]{3,2,1,0:T(8,128)(2,1)S(1)}, bf16[2,8,256,128]{3,2,1,0:T(8,128)(2,1)S(1)}, f32[256,1024]{1,0:T...) conditional(s32[]{:T(128)} %convert_element_type.2, (f32[1024,1024]{1,0:T(8,128)}, ...), branch_computations={%region_0.0_spmd, %region_1.0_spmd} | conditional | flops 25232932864 | bytes 40960108 | solution.py:465
  0.7 1.9 spread_first.1
  2.6 11.5 %all-to-all-start = ((f32[64,8,512]{2,1,0:T(8,128)}), f32[64,8,512]{2,1,0:T(8,128)S(1)}, u32[]{:S(2)}, u32[]{:S(2)}) async-start(f32[64,8,512]{2,1,0:T(8,128)} %spread_first.1), calls=%async_computation | async-start | bytes 2097152 | tf_op jit(solution)/shard_map/cond/branch_1_fun/all_to_all | solution.py:431
  14.1 7.3 %split.3 = (bf16[2,8,1024,128]{3,2,1,0:T(8,128)(2,1)}, bf16[2,8,1024,128]{3,2,1,0:T(8,128)(2,1)}) custom-call(f32[1024,1024]{1,0:T(8,128)} %get-tuple-element.49.refs_0_, f32[1024,1024]{1,0:T(8,128)} %get-tuple-element.50.refs_1_), custom_call_target="tpu_custom_call" | custom-call | flops 17179869184 | bytes 16777216 | tf_op jit(solution)/shard_map/cond/branch_1_fun/split/pallas_call | solution.py:160
  21.4 7.0 %all-to-all-done.blocks_ref = f32[64,8,512]{2,1,0:T(8,128)S(1)} async-done(((f32[64,8,512]{2,1,0:T(8,128)}), f32[64,8,512]{2,1,0:T(8,128)S(1)}, u32[]{:S(2)}, u32[]{:S(2)}) %all-to-all-start) | async-done | bytes 1048608 | tf_op jit(solution)/shard_map/cond/branch_1_fun/all_to_all | solution.py:431
  28.4 12.7 %forward_first.1 = (f32[64,8,1024]{2,1,0:T(8,128)S(1)}, bf16[2,8,256,128]{3,2,1,0:T(8,128)(2,1)S(1)}, bf16[2,8,256,128]{3,2,1,0:T(8,128)(2,1)S(1)}, f32[256,1024]{1,0:T(8,128)}) custom-call(f32[64,8,512]{2,1,0:T(8,128)S(1)} %all-to-all-done.blocks_ref, bf16[2,8,1024,128]{3,2,1,0:T(8,128)(2,1)} %get-tuple-element.124.wi_hbm, ...), custom_call_target="tpu_custom_call" | custom-call | flops 8053063680 | bytes 16777216 | tf_op jit(solution)/shard_map/cond/branch_1_fun/forward_first/pallas_call | solution.py:316
  41.1 0.0 copy-start
  41.1 24.3 %all_to_all.28.blocks_ref = f32[64,8,1024]{2,1,0:T(8,128)S(1)} all-to-all(f32[64,8,1024]{2,1,0:T(8,128)S(1)} %get-tuple-element.55), channel_id=1, replica_groups=mesh['segment'=2,'mp'=64] {'mp'}, dimensions={0} | all-to-all | bytes 4194304 | tf_op jit(solution)/shard_map/cond/branch_1_fun/all_to_all | solution.py:431
  65.5 0.0 copy-done
  65.5 0.1 sum_first.1
  65.6 1.3 collective-permute-start
  66.9 0.8 collective-permute-done
  67.7 0.0 copy-done.2
  67.7 2.7 %conditional.4 = (f32[4,1024]{1,0:T(4,128)S(1)}, f32[64,8,512]{2,1,0:T(8,128)}, f32[256,1024]{1,0:T(8,128)}, bf16[2,2,1024,128]{3,2,1,0:T(8,128)(2,1)}, bf16[2,2,1024,128]{3,2,1,0:T(8,128)(2,1)}) conditional(s32[]{:T(128)} %convert_element_type.2, (f32[4,2048]{1,0:T(4,128)S(1)}, f32[1,1024]{1,0:T(1,128)}, bf16[2,8,1024,128]{3,2,1,0:T(8,128)(2,1)}, ...), branch_computations={%region_2.0_spmd, %region_3.0_spmd} | conditional | flops 28454158336 | bytes 91242688 | solution.py:481
  67.7 1.6 turn.3
  69.4 1.1 broadcast.14
  70.4 1.3 collective-permute-start.1
  71.7 95.0 %collective-permute-done.1 = f32[4,1024]{1,0:T(4,128)S(1)} collective-permute-done((f32[4,1024]{1,0:T(4,128)S(1)}, f32[4,1024]{1,0:T(4,128)S(1)}, u32[]{:S(2)}, u32[]{:S(2)}) %collective-permute-start.1) | collective-permute-done | bytes 16416 | tf_op jit(solution)/shard_map/ppermute | solution.py:482
  166.8 19.1 %conditional.5 = (f32[64,8,512]{2,1,0:T(8,128)}) conditional(s32[]{:T(128)} %convert_element_type.2, f32[64,8,512]{2,1,0:T(8,128)} %get-tuple-element.103, f32[4,1024]{1,0:T(4,128)S(1)} %collective-permute-done.1), branch_computations={%region_4.0_spmd, %region_5.0_spmd} | conditional | bytes 2097160 | solution.py:490
  166.8 0.1 spread.1
  166.9 18.9 %all_to_all.32 = f32[64,8,512]{2,1,0:T(8,128)} all-to-all(f32[64,8,512]{2,1,0:T(8,128)S(1)} %spread.1), channel_id=1, replica_groups=mesh['segment'=2,'mp'=64] {'mp'}, dimensions={0} | all-to-all | bytes 2097152 | tf_op jit(solution)/shard_map/cond/branch_1_fun/all_to_all | solution.py:431
  185.8 10.3 %finish.1 = (f32[1024,1024]{1,0:T(8,128)}, f32[1024,1024]{1,0:T(8,128)}) custom-call(f32[64,8,512]{2,1,0:T(8,128)} %get-tuple-element.136.blocks_hbm, f32[256,1024]{1,0:T(8,128)} %get-tuple-element.105.p_hbm, f32[1024,1024]{1,0:T(8,128)} %bitcast.15, bf16[2,2,1024,128]{3,2,1,0:T(8,128)(2,1)} %get-tuple-element.106.at_hbm, ...), custom_call_target="tpu_custom_call" | custom-call | flops 4831838208 | bytes 12582912 | tf_op jit(solution)/shard_map/finish/pallas_call | solution.py:406
  (1 shorter events, 0.0 us)
Async XLA Ops:
  0.6 67.1 %copy-start.2 = (f32[2,2,1024]{2,1,0:T(2,128)S(1)}, f32[2,2,1024]{2,1,0:T(2,128)}, u32[]{:S(2)}) copy-start(f32[2,2,1024]{2,1,0:T(2,128)} %param.14) | copy-start | bytes 49156
  2.6 25.9 %all-to-all-start = ((f32[64,8,512]{2,1,0:T(8,128)}), f32[64,8,512]{2,1,0:T(8,128)S(1)}, u32[]{:S(2)}, u32[]{:S(2)}) async-start(f32[64,8,512]{2,1,0:T(8,128)} %spread_first.1), calls=%async_computation | async-start | bytes 2097152 | tf_op jit(solution)/shard_map/cond/branch_1_fun/all_to_all | solution.py:431
  41.1 24.3 %copy-start = (f32[2,2,1024]{2,1,0:T(2,128)S(1)}, f32[2,2,1024]{2,1,0:T(2,128)}, u32[]{:S(2)}) copy-start(f32[2,2,1024]{2,1,0:T(2,128)} %get-tuple-element.111.tok_ref) | copy-start | bytes 49156 | tf_op jit(solution)/shard_map/cond
  65.6 2.1 %collective-permute-start = (f32[4,2048]{1,0:T(4,128)S(1)}, f32[4,2048]{1,0:T(4,128)S(1)}, u32[]{:S(2)}, u32[]{:S(2)}) collective-permute-start(f32[4,2048]{1,0:T(4,128)S(1)} %get-tuple-element.97), channel_id=1, source_target_pairs={{0,64},{1,65},{2,66},{3,67},{4,68},{5,69},{6,70},{7,71},{8,72},{9,... | collective-permute-start | bytes 98312 | tf_op jit(solution)/shard_map/ppermute | solution.py:466
  70.4 96.3 %collective-permute-start.1 = (f32[4,1024]{1,0:T(4,128)S(1)}, f32[4,1024]{1,0:T(4,128)S(1)}, u32[]{:S(2)}, u32[]{:S(2)}) collective-permute-start(f32[4,1024]{1,0:T(4,128)S(1)} %get-tuple-element.104), channel_id=1, source_target_pairs={{64,0},{65,1},{66,2},{67,3},{68,4},{69,5},{70,6},{71,7},{72,8},{73... | collective-permute-start | bytes 49160 | tf_op jit(solution)/shard_map/ppermute | solution.py:482
